TPU v7x, 32 devices: a whole 2x2x4 slice. The times are simulated.
32 devices in a mesh: gx: 8 (over z, y), gy: 4 (over x, core).
Axes of the slice: x: 2, y: 2, z: 4, core: 2. Of those that a mesh axis runs over, the one named last changes fastest.
Arguments:
- prev_voltage: float32 [32, 32, 128, 128], P('gx', 'gy'), may hold values from -6 to 6
- source: float32 [32, 32, 128, 128], P('gx', 'gy'), may hold values from -30 to 30
- cap_over_h: float32 [32, 32, 128], P('gx', 'gy'), may hold values from 0.05 to 0.5
- diag_blocks: float32 [32, 32, 128, 128], P('gx', 'gy'), as said below
- inverse_blocks: float32 [32, 32, 128, 128], P('gx', 'gy'), as said below
- east_coupling: float32 [32, 32, 128, 128], P('gx', 'gy'), may hold values from 0 to 0.015625, as said below
- south_coupling: float32 [32, 32, 128, 128], P('gx', 'gy'), may hold values from 0 to 0.015625, as said below
- via_mask: int32 [32, 32, 2], P('gx', 'gy'), may hold values from 0 to 1, as said below
Outputs:
- voltage: float32 [32, 32, 128, 128], P('gx', 'gy')
- residual: float32 [32, 32, 128, 128], P('gx', 'gy')
Inputs may be any that keep to these rules, and one draw needn't show every extreme that they name: `via_mask`: 1 where the via coupling to the east (index 0) or south (index 1) neighbour block is present. `east_coupling`: nonnegative; zero in the last block column, which has no east neighbour. `south_coupling`: nonnegative; zero in the last block row, which has no south neighbour. `diag_blocks`: symmetric; off the diagonal nonpositive; each diagonal entry is cap_over_h plus the sum of the magnitudes of all other entries in its row of the system matrix, live couplings included. `inverse_blocks`: the inverse of the matching block of diag_blocks, in float32.
All inputs are finite; a program needn't handle non-finite values.
Results may differ from a plain program's by a relative error of at most 0.0003.
Values sent between devices are 32-bit elements; how exact they have to be, the bound alone decides.
A program may use at most 128 MiB of HBM per device.

v0:
```python
import functools

import jax
import jax.numpy as jnp
from jax import lax
from jax.experimental import pallas as pl
from jax.experimental.pallas import tpu as pltpu
from jax.sharding import PartitionSpec as P

ITERS = 4
STEPS = ITERS + 1
MESH = pl.DeviceIdType.MESH
F32, BF16 = jnp.float32, jnp.bfloat16


def ratio(num, den):
    return jnp.where(den == 0.0, 0.0, num / jnp.where(den == 0.0, 1.0, den))


def coefficients(moments):
    zero = jnp.zeros_like(moments[0])
    rho = [zero + 1.0] + [zero] * ITERS
    delta = [zero + 1.0] + [zero] * (ITERS - 1)
    xi = [zero] * ITERS
    gamma = moments[0]
    for k in range(ITERS):
        across = [(delta[i] if i < ITERS else zero) - (delta[i - 1] if i else zero) for i in range(k + 2)]
        curve = sum(delta[i] * across[j] * moments[i + j] for i in range(k + 1) for j in range(k + 2))
        alpha = ratio(gamma, curve)
        for i in range(k + 1):
            xi[i] = xi[i] + alpha * delta[i]
        for i in range(k + 2):
            rho[i] = rho[i] - alpha * across[i]
        if k + 1 < ITERS:
            later = sum(rho[i] * rho[j] * moments[i + j] for i in range(k + 2) for j in range(k + 2))
            beta = ratio(later, gamma)
            for i in range(k + 2):
                delta[i] = rho[i] + beta * delta[i]
            gamma = later
    return xi, rho


def halves(value):
    high = value.astype(BF16)
    low = (value - high.astype(F32)).astype(BF16)
    return jnp.concatenate([high, low], axis=1)


def times(left, right):
    stacked = jnp.concatenate([piece for piece in right for _ in range(2)], axis=0)
    wide = jnp.dot(left, stacked, preferred_element_type=F32)
    half = wide.shape[1] // 2
    return wide[:, :half] + wide[:, half:]


def kernel(
    nx, ny, paired,
    volt, source, cap, diag, inverse, east, south, mask,
    volt_out, res_out,
    U, T, X, L, PC, STE, ETE, HN, HD, HE, HW, PD, PE, RB, MOM, MR, G,
    load_sem, sN, rN, sD, rD, sR, rE, sP, rW, sB, rB, sG, rG,
):
    _, R, C, B, S = U.shape
    ix, iy = lax.axis_index("gx"), lax.axis_index("gy")
    north, south_on = ix > 0, ix < nx - 1
    west, east_on = iy > 0, iy < ny - 1

    loads = [
        pltpu.make_async_copy(src, dst, load_sem.at[n])
        for n, (src, dst) in enumerate(
            [(volt, U.at[0]), (south, T.at[2]), (east, T.at[1]), (inverse, T.at[3]), (diag, T.at[4]), (source, T.at[0])]
        )
    ]
    for load in loads:
        load.start()

    barrier = pltpu.get_barrier_semaphore()
    for d in range(1, nx):
        pl.semaphore_signal(barrier, inc=1, device_id={"gx": lax.rem(ix + d, nx)}, device_id_type=MESH)
    for d in range(1, ny):
        pl.semaphore_signal(barrier, inc=1, device_id={"gy": lax.rem(iy + d, ny)}, device_id_type=MESH)
    pl.semaphore_wait(barrier, nx + ny - 2)

    odd, nz = lax.rem(ix, 2) == 1, nx // 2
    AHEAD = min(3, C)
    EARLY = C - C // 4

    def place(c):
        return lax.rem(c + C - 1, C)

    def column(j):
        return lax.rem(j + 1, C)

    def long_south(z, c):
        return place(c) * nz < C * (nz - 1 - z)

    if paired:
        even = jnp.logical_not(odd)
        detour_south = lambda c: odd & long_south(lax.div(ix - 1, 2), c)
        detour_north = lambda c: even & jnp.logical_not(long_south(lax.div(ix, 2) - 1, c))
        passes_south = lambda c: even & (ix < nx - 2) & long_south(lax.div(ix, 2), c)
        passes_north = lambda c: odd & (ix > 2) & jnp.logical_not(long_south(lax.div(ix - 3, 2), c))

    def raw_north(k, c, far=False):
        src = volt.at[0, c] if k == 0 else U.at[k, 0, c]
        dst, sem, hop = (RB, rB, -1) if far else (HN, rN, 1)
        return pltpu.make_async_remote_copy(src, dst.at[k, c], sN.at[k, c], sem.at[k, c], device_id={"gx": ix - hop}, device_id_type=MESH)

    def product_south(k, c, far=False):
        dst, sem, hop = (RB, rB, -1) if far else (HD, rD, 1)
        return pltpu.make_async_remote_copy(PD.at[k, c], dst.at[k, c], sD.at[k, c], sem.at[k, c], device_id={"gx": ix + hop}, device_id_type=MESH)

    def start_raw(k, c):
        if not paired:
            raw_north(k, c).start()
            return
        far = detour_north(c)

        @pl.when(far)
        def _():
            raw_north(k, c, True).start()

        @pl.when(jnp.logical_not(far))
        def _():
            raw_north(k, c).start()

    def start_product(k, c):
        if not paired:
            product_south(k, c).start()
            return
        far = detour_south(c)

        @pl.when(far)
        def _():
            product_south(k, c, True).start()

        @pl.when(jnp.logical_not(far))
        def _():
            product_south(k, c).start()

    def onward(k, c, south):
        dst, sem, hop = (HD, rD, 2) if south else (HN, rN, -2)
        return pltpu.make_async_remote_copy(RB.at[k, c], dst.at[k, c], sB.at[k, c], sem.at[k, c], device_id={"gx": ix + hop}, device_id_type=MESH)

    def arrived(k, c):
        return pltpu.make_async_remote_copy(RB.at[k, c], RB.at[k, c], sB.at[k, c], rB.at[k, c], device_id={"gx": ix - 1}, device_id_type=MESH)

    def pass_south(k, c):
        if paired:
            @pl.when(passes_south(c))
            def _():
                arrived(k, c).wait_recv()
                onward(k, c, True).start()

    def pass_north(k, c):
        if paired:
            @pl.when(passes_north(c))
            def _():
                arrived(k, c).wait_recv()
                onward(k, c, False).start()

    def raw_west(k, r):
        src = volt.at[r, 0] if k == 0 else U.at[k, r, 0]
        return pltpu.make_async_remote_copy(src, HE.at[k, r], sR.at[k, r], rE.at[k, r], device_id={"gy": iy - 1}, device_id_type=MESH)

    def product_east(k, r):
        return pltpu.make_async_remote_copy(PE.at[k, r], HW.at[k, r], sP.at[k, r], rW.at[k, r], device_id={"gy": iy + 1}, device_id_type=MESH)

    @pl.when(north)
    def _():
        @pl.loop(0, AHEAD)
        def _(j):
            start_raw(0, column(j))

    @pl.when(west)
    def _():
        @pl.loop(0, R)
        def _(r):
            raw_west(0, r).start()

    def send_south(k, c):
        @pl.when(south_on)
        def _():
            PD[k, c] = times(STE[c], [X[k % 2, R, c + 1]])
            start_product(k, c)

    def send_side(k, r):
        @pl.when(east_on)
        def _():
            PE[k, r] = times(ETE[r], [X[k % 2, r + 1, C]])
            product_east(k, r).start()

        if k:
            @pl.when(west)
            def _():
                raw_west(k, r).start()

    MOM[...] = jnp.zeros_like(MOM)
    blank = jnp.zeros((B, 2 * S), BF16)
    for parity in range(2):
        for r in range(R + 2):
            X[parity, r, 0] = blank
            X[parity, r, C + 1] = blank
        for c in range(C + 2):
            X[parity, 0, c] = blank
            X[parity, R + 1, c] = blank
    for r in range(R):
        L[r, 0, :, 2 * B:4 * B] = blank
    for c in range(C):
        L[0, c, :, 6 * B:8 * B] = blank

    loads[0].wait()
    loads[1].wait()

    @pl.loop(0, C)
    def _(j):
        c = column(j)
        X[0, R, c + 1] = halves(U[0, R - 1, c])
        live = T[2, R - 1, c] * mask[R - 1, 1, c].astype(F32)
        STE[c] = halves(live.T)
        send_south(0, c)

        @pl.when(north & (j < C - AHEAD))
        def _():
            start_raw(0, column(j + AHEAD))

    loads[2].wait()

    @pl.loop(0, R)
    def _(r):
        X[0, r + 1, C] = halves(U[0, r, C - 1])
        live = T[1, r, C - 1] * mask[r, 0, C - 1].astype(F32)
        ETE[r] = halves(live.T)
        send_side(0, r)

    loads[3].wait()

    @pl.loop(0, R * C)
    def _(n):
        r, c = n // C, n % C

        X[0, r + 1, c + 1] = halves(U[0, r, c])
        PC[r, c] = halves(T[3, r, c])
        e_live = T[1, r, c] * mask[r, 0, c].astype(F32)
        L[r, c, :, 0:2 * B] = halves(e_live)
        s_live = T[2, r, c] * mask[r, 1, c].astype(F32)
        L[r, c, :, 4 * B:6 * B] = halves(s_live)

        @pl.when(c < C - 1)
        def _():
            L[r, c + 1, :, 2 * B:4 * B] = halves(e_live.T)

        @pl.when(r < R - 1)
        def _():
            L[r + 1, c, :, 6 * B:8 * B] = halves(s_live.T)

    loads[4].wait()
    loads[5].wait()

    def gather(m, former, latter):
        MOM[m] += jnp.sum((former * latter).reshape(B // 8, 8, S), axis=0)

    def image(k, r, c, extra=None):
        p = k % 2
        t = times(L[r, c], [X[p, r + 1, c + 2], X[p, r + 1, c], X[p, r + 2, c + 1], X[p, r, c + 1]])
        if extra is not None:
            for part in extra:
                t = t + part
        if k == 0:
            charge = jnp.broadcast_to(cap[r, pl.ds(c, 1), :], (S, B)).T
            t = t + (T[0, r, c] + charge * U[0, r, c]) - times(halves(T[4, r, c]), [X[0, r + 1, c + 1]])
        return t

    def finish(k, r, c, t):
        T[k, r, c] = t
        if k:
            gather(2 * k - 1, U[k, r, c], t)
        if k < ITERS:
            split = halves(t)
            u = times(PC[r, c], [split])
            U[k + 1, r, c] = u
            X[(k + 1) % 2, r + 1, c + 1] = halves(u)
            gather(2 * k, u, t)

    inner = list(range(1, R - 1))
    edges = [0] if R == 1 else [0, R - 1]
    def side_waits(k, rows):
        p = k % 2

        @pl.when(east_on)
        def _():
            for r in rows:
                raw_west(k, r).wait_recv()
                X[p, r + 1, C + 1] = halves(HE[k, r])

        @pl.when(west)
        def _():
            for r in rows:
                product_east(k, r).wait_recv()

        @pl.when(jnp.logical_not(west))
        def _():
            for r in rows:
                HW[k, r] = jnp.zeros((B, S), F32)

    def edge(k, c, side):
        p = k % 2

        if k < ITERS:
            @pl.when(south_on)
            def _():
                raw_north(k, c).wait_recv()
                X[p, R + 1, c + 1] = halves(HN[k, c])
        else:
            X[p, R + 1, c + 1] = blank

        @pl.when(north)
        def _():
            product_south(k, c).wait_recv()

        @pl.when(jnp.logical_not(north))
        def _():
            HD[k, c] = jnp.zeros((B, S), F32)

        first = (c == 0).astype(F32)
        ts = [
            image(k, r, c, ([first * HW[k, r]] if side else []) + ([HD[k, c]] if r == 0 else []))
            for r in edges
        ]
        for r, t in zip(edges, ts):
            finish(k, r, c, t)
        if k < ITERS:
            if k + 1 < ITERS:
                @pl.when(north)
                def _():
                    start_raw(k + 1, c)

            send_south(k + 1, c)
        else:
            gather(2 * k - 1, U[k, 0, c], HD[k, c])

    def passes(k, first, last):
        @pl.loop(first, last)
        def _(j):
            pass_south(k, column(j))
            if k < ITERS:
                pass_north(k, column(j))

    soon = (C // 4, C // 2)
    for k in range(STEPS):
        if k == 0:
            passes(k, 0, soon[0])

        @pl.loop(1, C - 1)
        def _(c):
            ts = [image(k, r, c) for r in inner]
            for r, t in zip(inner, ts):
                finish(k, r, c, t)

        if k == 0:
            passes(k, soon[0], soon[1])

        side_waits(k, inner)
        ts = [image(k, r, C - 1) for r in inner] + [image(k, r, 0, [HW[k, r]]) for r in inner]
        for n, t in enumerate(ts):
            r, c = (inner[n], C - 1) if n < len(inner) else (inner[n - len(inner)], 0)
            finish(k, r, c, t)
        if k < ITERS:
            for r in inner:
                send_side(k + 1, r)

        def passing(j):
            @pl.when(j >= (soon[1] if k == 0 else 0))
            def _():
                pass_south(k, column(j))
                if k < ITERS:
                    pass_north(k, column(j))

        @pl.loop(0, C - 2)
        def _(j):
            edge(k, column(j), False)
            passing(j)

        side_waits(k, edges)

        @pl.loop(C - 2, C)
        def _(j):
            edge(k, column(j), True)
            passing(j)

        if k < ITERS:
            for r in edges:
                send_side(k + 1, r)
        if k + 1 == ITERS:
            @pl.when(north)
            def _():
                @pl.loop(0, EARLY)
                def _(j):
                    start_raw(ITERS, column(j))

    def sent(k):
        @pl.loop(0, C)
        def _(c):
            @pl.when(north)
            def _():
                raw_north(k, c).wait_send()

            @pl.when(south_on)
            def _():
                product_south(k, c).wait_send()

            if paired:
                @pl.when(passes_south(c) | passes_north(c))
                def _():
                    onward(k, c, True).wait_send()

        @pl.loop(0, R)
        def _(r):
            @pl.when(west)
            def _():
                raw_west(k, r).wait_send()

            @pl.when(east_on)
            def _():
                product_east(k, r).wait_send()

    MR[0] = jnp.sum(MOM[...], axis=1)
    base = 0
    for stage, (axis, size, me) in enumerate((("gy", ny, iy), ("gx", nx, ix))):
        copies = []
        for d in range(1, size):
            copies.append(pltpu.make_async_remote_copy(
                MR.at[stage], G.at[base + me], sG.at[base + d], rG.at[base + d],
                device_id={axis: lax.rem(me + d, size)}, device_id_type=MESH))
        for copy in copies:
            copy.start()
        if stage:
            @pl.when(north)
            def _():
                @pl.loop(EARLY, C)
                def _(j):
                    start_raw(ITERS, column(j))

            @pl.loop(0, EARLY)
            def _(j):
                pass_north(ITERS, column(j))

            for k in range(ITERS):
                sent(k)
        G[base + me] = MR[stage]
        for copy in copies:
            copy.wait()
        total = G[base]
        for d in range(1, size):
            total = total + G[base + d]
        MR[stage + 1] = total
        base += size

    @pl.loop(EARLY, C)
    def _(j):
        pass_north(ITERS, column(j))

    summed = MR[2]
    xi, rho = coefficients([summed[m:m + 1] for m in range(2 * ITERS)])

    for r in range(R):
        @pl.loop(0, C)
        def _(c):
            v = U[0, r, c]
            for i in range(ITERS):
                v = v + xi[i] * U[i + 1, r, c]
            volt_out[r, c] = v
            w = rho[0] * T[0, r, c]
            for i in range(1, STEPS):
                w = w + rho[i] * T[i, r, c]
            res_out[r, c] = w

    @pl.when(south_on)
    def _():
        @pl.loop(0, C)
        def _(j):
            c = column(j)
            raw_north(ITERS, c).wait_recv()
            late = times(L[R - 1, c, :, 4 * B:6 * B], [halves(HN[ITERS, c])])
            res_out[R - 1, c] = res_out[R - 1, c] + rho[ITERS] * late

    sent(ITERS)


def shards(nx, ny, paired, volt, source, cap, diag, inverse, east, south, mask):
    R, C, B, S = volt.shape
    mask = jnp.swapaxes(mask, 1, 2)
    hbm = pl.BlockSpec(memory_space=pl.ANY)
    vmem = pl.BlockSpec(memory_space=pltpu.VMEM)
    smem = pl.BlockSpec(memory_space=pltpu.SMEM)
    dma = pltpu.SemaphoreType.DMA
    shape = pltpu.VMEM(volt.shape, F32)
    return pl.pallas_call(
        functools.partial(kernel, nx, ny, paired),
        out_shape=(shape, shape),
        in_specs=[hbm, hbm, vmem, hbm, hbm, hbm, hbm, smem],
        out_specs=(vmem, vmem),
        scratch_shapes=[
            pltpu.VMEM((STEPS, R, C, B, S), F32),
            pltpu.VMEM((STEPS, R, C, B, S), F32),
            pltpu.VMEM((2, R + 2, C + 2, B, 2 * S), BF16),
            pltpu.VMEM((R, C, B, 8 * B), BF16),
            pltpu.VMEM((R, C, B, 2 * B), BF16),
            pltpu.VMEM((C, B, 2 * B), BF16),
            pltpu.VMEM((R, B, 2 * B), BF16),
            pltpu.VMEM((STEPS, C, B, S), F32),
            pltpu.VMEM((STEPS, C, B, S), F32),
            pltpu.VMEM((STEPS, R, B, S), F32),
            pltpu.VMEM((STEPS, R, B, S), F32),
            pltpu.VMEM((STEPS, C, B, S), F32),
            pltpu.VMEM((STEPS, R, B, S), F32),
            pltpu.VMEM((STEPS, C, B, S), F32),
            pltpu.VMEM((2 * ITERS, 8, S), F32),
            pltpu.VMEM((3, 2 * ITERS, S), F32),
            pltpu.VMEM((nx + ny, 2 * ITERS, S), F32),
            dma((6,)),
            dma((STEPS, C)), dma((STEPS, C)),
            dma((STEPS, C)), dma((STEPS, C)),
            dma((STEPS, R)), dma((STEPS, R)),
            dma((STEPS, R)), dma((STEPS, R)),
            dma((STEPS, C)), dma((STEPS, C)),
            dma((nx + ny,)), dma((nx + ny,)),
        ],
        compiler_params=pltpu.CompilerParams(
            collective_id=0, has_side_effects=True, vmem_limit_bytes=58 * 1024 * 1024
        ),
    )(volt, source, cap, diag, inverse, east, south, mask)


def two_rows(mesh):
    places = [getattr(d, "coords", None) for d in mesh.devices[:, 0]]
    if None in places or len(places) % 2 or len(places) < 4:
        return False
    hops = [sum(abs(int(p) - int(q)) for p, q in zip(a, b)) for a, b in zip(places, places[1:])]
    return all(hop == 1 + i % 2 for i, hop in enumerate(hops))


def solution(mesh):
    grid = P("gx", "gy", None, None)
    in_specs = (grid, grid, P("gx", "gy", None), grid, grid, grid, grid, P("gx", "gy", None))
    body = functools.partial(shards, mesh.shape["gx"], mesh.shape["gy"], two_rows(mesh))
    return jax.shard_map(body, mesh=mesh, in_specs=in_specs, out_specs=(grid, grid), check_vma=False)
```

profile of v0, /device:TPU:0, one launch (start us, length us, event | category | flops | bytes accessed | tf_op | source)
XLA Modules:
  0.0 122.4 jit_solution(8335422299869213954)
XLA Ops:
  0.6 119.2 %shard_map.95 = (f32[4,8,128,128]{3,2,1,0:T(8,128)S(1)}, f32[4,8,128,128]{3,2,1,0:T(8,128)S(1)}) custom-call(f32[4,8,128,128]{3,2,1,0:T(8,128)} %volt.1, f32[4,8,128,128]{3,2,1,0:T(8,128)} %source.1, f32[4,8,128]{2,1,0:T(8,128)} %cap.1, f32[4,8,128,128]{3,2,1,0:T(8,128)} %diag.1, f32[4,8,128,128]{3,2,1,0:T(8,128)} %inverse.1, f32[4,8,128,128]{3,2,1,0:T(8,128)} %east.1, ...), custom_call_target="tpu_custom_call" | custom-call | tf_op jit(solution)/shard_map/pallas_call | solution.py:498
  119.8 1.3 %copy.12 = f32[4,8,128,128]{3,2,1,0:T(8,128)} copy(f32[4,8,128,128]{3,2,1,0:T(8,128)S(1)} %get-tuple-element.2) | data formatting | bytes 4194304
  121.1 1.3 %copy.13 = f32[4,8,128,128]{3,2,1,0:T(8,128)} copy(f32[4,8,128,128]{3,2,1,0:T(8,128)S(1)} %get-tuple-element.3) | data formatting | bytes 4194304
where the time goes:
time: 123 us; the launch traced here: 122 us
  Pallas kernels  119 us (97%)
  local copies, waits for them, and re-layouts  2.64 us (2%)
    pallas_call x1, Pallas kernels, shards(): pl.pallas_call(functools.partial(kernel, nx, ny, paired), out_shape=(shap...  119 us
    unnamed x2, local copies, waits for them, and re-layouts  2.64 us

commit v1 on v0

--- a/solution.py
+++ b/solution.py
@@ -17,7 +17,7 @@
     return jnp.where(den == 0.0, 0.0, num / jnp.where(den == 0.0, 1.0, den))
 
 
-def coefficients(moments):
+def before_last(moments):
     zero = jnp.zeros_like(moments[0])
     rho = [zero + 1.0] + [zero] * ITERS
     delta = [zero + 1.0] + [zero] * (ITERS - 1)
@@ -25,19 +25,22 @@
     gamma = moments[0]
     for k in range(ITERS):
         across = [(delta[i] if i < ITERS else zero) - (delta[i - 1] if i else zero) for i in range(k + 2)]
-        curve = sum(delta[i] * across[j] * moments[i + j] for i in range(k + 1) for j in range(k + 2))
+        curve = sum(
+            delta[i] * across[j] * moments[i + j]
+            for i in range(k + 1) for j in range(k + 2) if i + j < len(moments)
+        )
+        if k + 1 == ITERS:
+            return xi, delta, rho, across, gamma, curve
         alpha = ratio(gamma, curve)
         for i in range(k + 1):
             xi[i] = xi[i] + alpha * delta[i]
         for i in range(k + 2):
             rho[i] = rho[i] - alpha * across[i]
-        if k + 1 < ITERS:
-            later = sum(rho[i] * rho[j] * moments[i + j] for i in range(k + 2) for j in range(k + 2))
-            beta = ratio(later, gamma)
-            for i in range(k + 2):
-                delta[i] = rho[i] + beta * delta[i]
-            gamma = later
-    return xi, rho
+        later = sum(rho[i] * rho[j] * moments[i + j] for i in range(k + 2) for j in range(k + 2))
+        beta = ratio(later, gamma)
+        for i in range(k + 2):
+            delta[i] = rho[i] + beta * delta[i]
+        gamma = later
 
 
 def halves(value):
@@ -56,9 +59,9 @@
 def kernel(
     nx, ny, paired,
     volt, source, cap, diag, inverse, east, south, mask,
-    volt_out, res_out,
-    U, T, X, L, PC, STE, ETE, HN, HD, HE, HW, PD, PE, RB, MOM, MR, G,
-    load_sem, sN, rN, sD, rD, sR, rE, sP, rW, sB, rB, sG, rG,
+    volt_out, dir_out, res_out, img_out, step_out,
+    U, T, X, L, PC, STE, ETE, HN, HD, HE, HW, PD, PE, RB, MOM, G, F,
+    load_sem, sN, rN, sD, rD, sR, rE, sP, rW, sB, rB, sG, sF, here,
 ):
     _, R, C, B, S = U.shape
     ix, iy = lax.axis_index("gx"), lax.axis_index("gy")
@@ -80,10 +83,13 @@
     for d in range(1, ny):
         pl.semaphore_signal(barrier, inc=1, device_id={"gy": lax.rem(iy + d, ny)}, device_id_type=MESH)
     pl.semaphore_wait(barrier, nx + ny - 2)
+    for d in range(1, ny):
+        pl.semaphore_signal(here, inc=1, device_id={"gy": lax.rem(iy + d, ny)}, device_id_type=MESH)
 
     odd, nz = lax.rem(ix, 2) == 1, nx // 2
     AHEAD = min(3, C)
     EARLY = C - C // 4
+    HOLD = C // 2
 
     def place(c):
         return lax.rem(c + C - 1, C)
@@ -104,46 +110,65 @@
     def raw_north(k, c, far=False):
         src = volt.at[0, c] if k == 0 else U.at[k, 0, c]
         dst, sem, hop = (RB, rB, -1) if far else (HN, rN, 1)
-        return pltpu.make_async_remote_copy(src, dst.at[k, c], sN.at[k, c], sem.at[k, c], device_id={"gx": ix - hop}, device_id_type=MESH)
+        return pltpu.make_async_remote_copy(src, dst.at[k, c], sN, sem.at[k % 2, c], device_id={"gx": ix - hop}, device_id_type=MESH)
 
     def product_south(k, c, far=False):
         dst, sem, hop = (RB, rB, -1) if far else (HD, rD, 1)
-        return pltpu.make_async_remote_copy(PD.at[k, c], dst.at[k, c], sD.at[k, c], sem.at[k, c], device_id={"gx": ix + hop}, device_id_type=MESH)
-
-    def start_raw(k, c):
+        return pltpu.make_async_remote_copy(PD.at[k, c], dst.at[k, c], sD, sem.at[k % 2, c], device_id={"gx": ix + hop}, device_id_type=MESH)
+
+    def start_raw(k, c, own=True, through=True):
         if not paired:
-            raw_north(k, c).start()
+            if own:
+                raw_north(k, c).start()
             return
         far = detour_north(c)
-
-        @pl.when(far)
-        def _():
-            raw_north(k, c, True).start()
-
-        @pl.when(jnp.logical_not(far))
-        def _():
-            raw_north(k, c).start()
-
-    def start_product(k, c):
+        if own:
+            @pl.when(north & far)
+            def _():
+                raw_north(k, c, True).start()
+
+            @pl.when(north & odd)
+            def _():
+                raw_north(k, c).start()
+        if through:
+            @pl.when(north & even & jnp.logical_not(far))
+            def _():
+                raw_north(k, c).start()
+
+    def start_product(k, c, own=True, through=True):
         if not paired:
-            product_south(k, c).start()
+            if own:
+                product_south(k, c).start()
             return
         far = detour_south(c)
-
-        @pl.when(far)
-        def _():
-            product_south(k, c, True).start()
-
-        @pl.when(jnp.logical_not(far))
-        def _():
-            product_south(k, c).start()
+        if own:
+            @pl.when(far)
+            def _():
+                product_south(k, c, True).start()
+
+            @pl.when(even)
+            def _():
+                product_south(k, c).start()
+        if through:
+            @pl.when(odd & jnp.logical_not(far))
+            def _():
+                product_south(k, c).start()
+
+    def start_through(k, c):
+        if paired:
+            if k < ITERS:
+                start_raw(k, c, own=False)
+            if k:
+                @pl.when(south_on)
+                def _():
+                    start_product(k, c, own=False)
 
     def onward(k, c, south):
         dst, sem, hop = (HD, rD, 2) if south else (HN, rN, -2)
-        return pltpu.make_async_remote_copy(RB.at[k, c], dst.at[k, c], sB.at[k, c], sem.at[k, c], device_id={"gx": ix + hop}, device_id_type=MESH)
+        return pltpu.make_async_remote_copy(RB.at[k, c], dst.at[k, c], sB.at[k], sem.at[k % 2, c], device_id={"gx": ix + hop}, device_id_type=MESH)
 
     def arrived(k, c):
-        return pltpu.make_async_remote_copy(RB.at[k, c], RB.at[k, c], sB.at[k, c], rB.at[k, c], device_id={"gx": ix - 1}, device_id_type=MESH)
+        return pltpu.make_async_remote_copy(RB.at[k, c], RB.at[k, c], sB.at[k], rB.at[k % 2, c], device_id={"gx": ix - 1}, device_id_type=MESH)
 
     def pass_south(k, c):
         if paired:
@@ -161,10 +186,10 @@
 
     def raw_west(k, r):
         src = volt.at[r, 0] if k == 0 else U.at[k, r, 0]
-        return pltpu.make_async_remote_copy(src, HE.at[k, r], sR.at[k, r], rE.at[k, r], device_id={"gy": iy - 1}, device_id_type=MESH)
+        return pltpu.make_async_remote_copy(src, HE.at[k, r], sR, rE.at[k % 2, r], device_id={"gy": iy - 1}, device_id_type=MESH)
 
     def product_east(k, r):
-        return pltpu.make_async_remote_copy(PE.at[k, r], HW.at[k, r], sP.at[k, r], rW.at[k, r], device_id={"gy": iy + 1}, device_id_type=MESH)
+        return pltpu.make_async_remote_copy(PE.at[k, r], HW.at[k, r], sP, rW.at[k % 2, r], device_id={"gy": iy + 1}, device_id_type=MESH)
 
     @pl.when(north)
     def _():
@@ -182,7 +207,7 @@
         @pl.when(south_on)
         def _():
             PD[k, c] = times(STE[c], [X[k % 2, R, c + 1]])
-            start_product(k, c)
+            start_product(k, c, through=k == 0)
 
     def send_side(k, r):
         @pl.when(east_on)
@@ -330,26 +355,47 @@
         for r, t in zip(edges, ts):
             finish(k, r, c, t)
         if k < ITERS:
-            if k + 1 < ITERS:
-                @pl.when(north)
+            raws = k + 1 < ITERS
+            if raws:
+                @pl.when(north & jnp.logical_not(odd))
                 def _():
-                    start_raw(k + 1, c)
+                    start_raw(k + 1, c, through=False)
 
             send_south(k + 1, c)
+            if raws:
+                @pl.when(north & odd)
+                def _():
+                    start_raw(k + 1, c, through=False)
         else:
             gather(2 * k - 1, U[k, 0, c], HD[k, c])
 
-    def passes(k, first, last):
-        @pl.loop(first, last)
-        def _(j):
-            pass_south(k, column(j))
-            if k < ITERS:
-                pass_north(k, column(j))
-
-    soon = (C // 4, C // 2)
+    me, count = ix * ny + iy, nx * ny
+
+    def spread(ref, sems):
+        @pl.loop(1, count)
+        def _(d):
+            other = lax.rem(me + d, count)
+            pltpu.make_async_remote_copy(
+                ref.at[me], ref.at[me], sems.at[0], sems.at[1],
+                device_id={"gx": lax.div(other, ny), "gy": lax.rem(other, ny)}, device_id_type=MESH).start()
+
+    def spreading(ref, sems):
+        others = ref.at[pl.ds(0, count - 1)]
+        return pltpu.make_async_remote_copy(others, others, sems.at[0], sems.at[1], device_id={"gx": ix}, device_id_type=MESH)
+
+    def now(j):
+        return (j < EARLY) | jnp.logical_not(odd) if paired else j < EARLY
+
+    def pass_on(k, c):
+        pass_south(k, c)
+        if k < ITERS:
+            pass_north(k, c)
+
     for k in range(STEPS):
         if k == 0:
-            passes(k, 0, soon[0])
+            @pl.loop(0, C // 4)
+            def _(j):
+                pass_on(k, column(j))
 
         @pl.loop(1, C - 1)
         def _(c):
@@ -358,7 +404,9 @@
                 finish(k, r, c, t)
 
         if k == 0:
-            passes(k, soon[0], soon[1])
+            @pl.loop(C // 4, C // 2)
+            def _(j):
+                pass_on(k, column(j))
 
         side_waits(k, inner)
         ts = [image(k, r, C - 1) for r in inner] + [image(k, r, 0, [HW[k, r]]) for r in inner]
@@ -369,111 +417,104 @@
             for r in inner:
                 send_side(k + 1, r)
 
-        def passing(j):
-            @pl.when(j >= (soon[1] if k == 0 else 0))
-            def _():
-                pass_south(k, column(j))
+        if k == ITERS:
+            @pl.when(north)
+            def _():
+                @pl.loop(0, C)
+                def _(j):
+                    @pl.when(now(j))
+                    def _():
+                        start_raw(ITERS, column(j), through=False)
+        elif k:
+            @pl.loop(C - HOLD, C)
+            def _(j):
+                start_through(k, column(j))
+
+        lead = C // 2 if k == 0 else 0
+
+        def held(j):
+            @pl.when(j >= HOLD)
+            def _():
                 if k < ITERS:
-                    pass_north(k, column(j))
+                    start_through(k + 1, column(j - HOLD))
+                elif paired:
+                    start_raw(k, column(j - HOLD), own=False)
 
         @pl.loop(0, C - 2)
         def _(j):
+            @pl.when(j + lead < C)
+            def _():
+                pass_on(k, column(j + lead))
+
             edge(k, column(j), False)
-            passing(j)
+            held(j)
 
         side_waits(k, edges)
 
         @pl.loop(C - 2, C)
         def _(j):
+            if not lead:
+                pass_on(k, column(j))
             edge(k, column(j), True)
-            passing(j)
+            held(j)
 
         if k < ITERS:
             for r in edges:
                 send_side(k + 1, r)
         if k + 1 == ITERS:
-            @pl.when(north)
-            def _():
-                @pl.loop(0, EARLY)
-                def _(j):
-                    start_raw(ITERS, column(j))
-
-    def sent(k):
-        @pl.loop(0, C)
-        def _(c):
-            @pl.when(north)
-            def _():
-                raw_north(k, c).wait_send()
-
-            @pl.when(south_on)
-            def _():
-                product_south(k, c).wait_send()
-
-            if paired:
-                @pl.when(passes_south(c) | passes_north(c))
-                def _():
-                    onward(k, c, True).wait_send()
-
-        @pl.loop(0, R)
-        def _(r):
-            @pl.when(west)
-            def _():
-                raw_west(k, r).wait_send()
-
-            @pl.when(east_on)
-            def _():
-                product_east(k, r).wait_send()
-
-    MR[0] = jnp.sum(MOM[...], axis=1)
-    base = 0
-    for stage, (axis, size, me) in enumerate((("gy", ny, iy), ("gx", nx, ix))):
-        copies = []
-        for d in range(1, size):
-            copies.append(pltpu.make_async_remote_copy(
-                MR.at[stage], G.at[base + me], sG.at[base + d], rG.at[base + d],
-                device_id={axis: lax.rem(me + d, size)}, device_id_type=MESH))
-        for copy in copies:
-            copy.start()
-        if stage:
-            @pl.when(north)
-            def _():
-                @pl.loop(EARLY, C)
-                def _(j):
-                    start_raw(ITERS, column(j))
-
-            @pl.loop(0, EARLY)
+            pl.semaphore_wait(here, ny - 1)
+            @pl.loop(C - HOLD, C)
             def _(j):
-                pass_north(ITERS, column(j))
-
-            for k in range(ITERS):
-                sent(k)
-        G[base + me] = MR[stage]
-        for copy in copies:
-            copy.wait()
-        total = G[base]
-        for d in range(1, size):
-            total = total + G[base + d]
-        MR[stage + 1] = total
-        base += size
-
-    @pl.loop(EARLY, C)
+                start_through(ITERS, column(j))
+
+            G[me] = jnp.sum(MOM[...], axis=1)
+            spread(G, sG)
+
+    F[me] = jnp.sum(MOM[2 * ITERS - 1], axis=0, keepdims=True)
+    spread(F, sF)
+
+    @pl.when(north)
+    def _():
+        @pl.loop(EARLY, C)
+        def _(j):
+            @pl.when(jnp.logical_not(now(j)))
+            def _():
+                start_raw(ITERS, column(j), through=False)
+
+        if paired:
+            @pl.loop(C - HOLD, C)
+            def _(j):
+                start_raw(ITERS, column(j), own=False)
+
+    @pl.loop(0, C // 2)
     def _(j):
         pass_north(ITERS, column(j))
 
-    summed = MR[2]
-    xi, rho = coefficients([summed[m:m + 1] for m in range(2 * ITERS)])
+    spreading(G, sG).wait_recv()
+    summed = jnp.sum(G[...], axis=0)
+    xi, delta, rho, across, gamma, curve = before_last([summed[m:m + 1] for m in range(2 * ITERS - 1)])
+
+    def mix(weights, terms):
+        total = None
+        for weight, term in zip(weights, terms):
+            total = weight * term if total is None else total + weight * term
+        return total
 
     for r in range(R):
         @pl.loop(0, C)
         def _(c):
-            v = U[0, r, c]
-            for i in range(ITERS):
-                v = v + xi[i] * U[i + 1, r, c]
-            volt_out[r, c] = v
-            w = rho[0] * T[0, r, c]
-            for i in range(1, STEPS):
-                w = w + rho[i] * T[i, r, c]
-            res_out[r, c] = w
+            us = [U[i + 1, r, c] for i in range(ITERS)]
+            ts = [T[i, r, c] for i in range(STEPS)]
+            volt_out[r, c] = U[0, r, c] + mix(xi[:ITERS - 1], us)
+            dir_out[r, c] = mix(delta, us)
+            res_out[r, c] = mix(rho[:ITERS], ts)
+            img_out[r, c] = mix(across, ts)
+
+        rest = C - C // 2
+
+        @pl.loop(C - rest + rest * r // R, C - rest + rest * (r + 1) // R)
+        def _(j):
+            pass_north(ITERS, column(j))
 
     @pl.when(south_on)
     def _():
@@ -482,9 +523,31 @@
             c = column(j)
             raw_north(ITERS, c).wait_recv()
             late = times(L[R - 1, c, :, 4 * B:6 * B], [halves(HN[ITERS, c])])
-            res_out[R - 1, c] = res_out[R - 1, c] + rho[ITERS] * late
-
-    sent(ITERS)
+            img_out[R - 1, c] = img_out[R - 1, c] + across[ITERS] * late
+
+    spreading(F, sF).wait_recv()
+    last = jnp.sum(F[...], axis=0)
+    step_out[...] = ratio(gamma, curve + delta[ITERS - 1] * across[ITERS] * last)
+    spreading(G, sG).wait_send()
+    spreading(F, sF).wait_send()
+
+    def sent(cond, ref, sem):
+        @pl.when(cond)
+        def _():
+            pltpu.make_async_remote_copy(ref, ref, sem, sem, device_id={"gx": ix}, device_id_type=MESH).wait_send()
+
+    sent(north, HN, sN)
+    sent(south_on, PD, sD)
+    sent(west, HE, sR)
+    sent(east_on, PE, sP)
+    if paired:
+        for z in range(nz - 1):
+            souths = -(-C * (nz - 1 - z) // nz)
+            for k in range(STEPS):
+                if souths:
+                    sent(ix == 2 * z, RB.at[k, pl.ds(0, souths)], sB.at[k])
+                if C - souths:
+                    sent(ix == 2 * z + 3, RB.at[k, pl.ds(0, C - souths)], sB.at[k])
 
 
 def shards(nx, ny, paired, volt, source, cap, diag, inverse, east, south, mask):
@@ -495,11 +558,11 @@
     smem = pl.BlockSpec(memory_space=pltpu.SMEM)
     dma = pltpu.SemaphoreType.DMA
     shape = pltpu.VMEM(volt.shape, F32)
-    return pl.pallas_call(
+    volt, direction, res, image, step = pl.pallas_call(
         functools.partial(kernel, nx, ny, paired),
-        out_shape=(shape, shape),
+        out_shape=(shape, shape, shape, shape, pltpu.VMEM((1, S), F32)),
         in_specs=[hbm, hbm, vmem, hbm, hbm, hbm, hbm, smem],
-        out_specs=(vmem, vmem),
+        out_specs=(vmem,) * 5,
         scratch_shapes=[
             pltpu.VMEM((STEPS, R, C, B, S), F32),
             pltpu.VMEM((STEPS, R, C, B, S), F32),
@@ -516,20 +579,21 @@
             pltpu.VMEM((STEPS, R, B, S), F32),
             pltpu.VMEM((STEPS, C, B, S), F32),
             pltpu.VMEM((2 * ITERS, 8, S), F32),
-            pltpu.VMEM((3, 2 * ITERS, S), F32),
-            pltpu.VMEM((nx + ny, 2 * ITERS, S), F32),
+            pltpu.VMEM((nx * ny, 2 * ITERS, S), F32),
+            pltpu.VMEM((nx * ny, 1, S), F32),
             dma((6,)),
-            dma((STEPS, C)), dma((STEPS, C)),
-            dma((STEPS, C)), dma((STEPS, C)),
-            dma((STEPS, R)), dma((STEPS, R)),
-            dma((STEPS, R)), dma((STEPS, R)),
-            dma((STEPS, C)), dma((STEPS, C)),
-            dma((nx + ny,)), dma((nx + ny,)),
+            dma, dma((2, C)),
+            dma, dma((2, C)),
+            dma, dma((2, R)),
+            dma, dma((2, R)),
+            dma((STEPS,)), dma((2, C)),
+            dma((2,)), dma((2,)), pltpu.SemaphoreType.REGULAR,
         ],
         compiler_params=pltpu.CompilerParams(
-            collective_id=0, has_side_effects=True, vmem_limit_bytes=58 * 1024 * 1024
+            collective_id=0, has_side_effects=True, vmem_limit_bytes=55 * 1024 * 1024
         ),
     )(volt, source, cap, diag, inverse, east, south, mask)
+    return volt + step * direction, res - step * image
 
 
 def two_rows(mesh):

time: 123 us -> 115 us (0.935)
  Pallas kernels: 119 us -> 110 us
  other arithmetic: 0 us -> 3.24 us
  local copies, waits for them, and re-layouts: 2.64 us -> 0 us
    pallas_call x1, Pallas kernels: 119 us -> 110 us  [shards(): pl.pallas_call(functools.partial(kernel, nx, ny, paired), out_shape=(shap...]
    sub x0 -> x1, other arithmetic: none -> 3.24 us  [shards(): return (volt + step * direction, res - step * image)]
    unnamed x2 -> x0, local copies, waits for them, and re-layouts: 2.64 us -> none
where the time goes in v1:
time: 115 us; the launch traced here: 114 us
  Pallas kernels  110 us (96%)
  other arithmetic  3.24 us (3%)
    pallas_call x1, Pallas kernels, shards(): pl.pallas_call(functools.partial(kernel, nx, ny, paired), out_shape=(shap...  110 us
    sub x1, other arithmetic, shards(): return (volt + step * direction, res - step * image)  3.24 us

profile of v1, /device:TPU:0, one launch (start us, length us, event | category | flops | bytes accessed | tf_op | source)
XLA Modules:
  0.0 114.3 jit_solution(15240708404711330328)
XLA Ops:
  0.6 110.4 %shard_map.95 = (f32[4,8,128,128]{3,2,1,0:T(8,128)S(1)}, f32[4,8,128,128]{3,2,1,0:T(8,128)S(1)}, f32[4,8,128,128]{3,2,1,0:T(8,128)S(1)}, f32[4,8,128,128]{3,2,1,0:T(8,128)S(1)}, f32[1,128]{1,0:T(1,128)S(1)}) custom-call(f32[4,8,128,128]{3,2,1,0:T(8,128)} %volt.1, f32[4,8,128,128]{3,2,1,0:T(8,128)} %source.1, f32[4,8,128]{2,1,0:T(8,128)} %cap.1, ...), custom_call_target="tpu_custom_call" | custom-call | tf_op jit(solution)/shard_map/pallas_call | solution.py:561
  111.1 3.2 %multiply_subtract_fusion = (f32[4,8,128,128]{3,2,1,0:T(8,128)}, f32[4,8,128,128]{3,2,1,0:T(8,128)}) fusion(f32[4,8,128,128]{3,2,1,0:T(8,128)S(1)} %get-tuple-element.10, f32[4,8,128,128]{3,2,1,0:T(8,128)S(1)} %get-tuple-element.11, f32[128]{0:T(128)S(1)} %bitcast.2, f32[4,8,128,128]{3,2,1,0:T(8,128)S(1)} %get-tuple-element.7, ...), kind=kLoop, calls=%fused_computation | loop fusion | flops 2097152 | bytes 12583424 | tf_op jit(solution)/shard_map/sub | solution.py:596

commit v2 on v1

--- a/solution.py
+++ b/solution.py
@@ -58,9 +58,9 @@
 
 def kernel(
     nx, ny, paired,
-    volt, source, cap, diag, inverse, east, south, mask,
+    volt, source, cap_in, diag, inverse, east, south, mask_in,
     volt_out, dir_out, res_out, img_out, step_out,
-    U, T, X, L, PC, STE, ETE, HN, HD, HE, HW, PD, PE, RB, MOM, G, F,
+    U, T, X, L, PC, STE, ETE, HN, HD, HE, HW, PD, PE, RB, MOM, G, F, cap, mask,
     load_sem, sN, rN, sD, rD, sR, rE, sP, rW, sB, rB, sG, sF, here,
 ):
     _, R, C, B, S = U.shape
@@ -71,7 +71,7 @@
     loads = [
         pltpu.make_async_copy(src, dst, load_sem.at[n])
         for n, (src, dst) in enumerate(
-            [(volt, U.at[0]), (south, T.at[2]), (east, T.at[1]), (inverse, T.at[3]), (diag, T.at[4]), (source, T.at[0])]
+            [(volt, U.at[0]), (south, T.at[2]), (east, T.at[1]), (inverse, T.at[3]), (diag, T.at[4]), (source, T.at[0]), (cap_in, cap), (mask_in, mask)]
         )
     ]
     for load in loads:
@@ -88,6 +88,7 @@
 
     odd, nz = lax.rem(ix, 2) == 1, nx // 2
     AHEAD = min(3, C)
+    TAIL = min(2, C - AHEAD)
     EARLY = C - C // 4
     HOLD = C // 2
 
@@ -196,6 +197,13 @@
         @pl.loop(0, AHEAD)
         def _(j):
             start_raw(0, column(j))
+
+        if paired:
+            @pl.loop(C - TAIL, C)
+            def _(j):
+                @pl.when(even)
+                def _():
+                    start_raw(0, column(j))
 
     @pl.when(west)
     def _():
@@ -234,6 +242,7 @@
     for c in range(C):
         L[0, c, :, 6 * B:8 * B] = blank
 
+    loads[7].wait()
     loads[0].wait()
     loads[1].wait()
 
@@ -245,7 +254,9 @@
         STE[c] = halves(live.T)
         send_south(0, c)
 
-        @pl.when(north & (j < C - AHEAD))
+        gone = even & (j + AHEAD >= C - TAIL) if paired else False
+
+        @pl.when(north & (j < C - AHEAD) & jnp.logical_not(gone))
         def _():
             start_raw(0, column(j + AHEAD))
 
@@ -281,6 +292,7 @@
 
     loads[4].wait()
     loads[5].wait()
+    loads[6].wait()
 
     def gather(m, former, latter):
         MOM[m] += jnp.sum((former * latter).reshape(B // 8, 8, S), axis=0)
@@ -417,15 +429,7 @@
             for r in inner:
                 send_side(k + 1, r)
 
-        if k == ITERS:
-            @pl.when(north)
-            def _():
-                @pl.loop(0, C)
-                def _(j):
-                    @pl.when(now(j))
-                    def _():
-                        start_raw(ITERS, column(j), through=False)
-        elif k:
+        if 0 < k < ITERS:
             @pl.loop(C - HOLD, C)
             def _(j):
                 start_through(k, column(j))
@@ -438,7 +442,9 @@
                 if k < ITERS:
                     start_through(k + 1, column(j - HOLD))
                 elif paired:
-                    start_raw(k, column(j - HOLD), own=False)
+                    @pl.when(ix < 4)
+                    def _():
+                        start_raw(k, column(j - HOLD), own=False)
 
         @pl.loop(0, C - 2)
         def _(j):
@@ -470,6 +476,14 @@
             G[me] = jnp.sum(MOM[...], axis=1)
             spread(G, sG)
 
+            @pl.when(north)
+            def _():
+                @pl.loop(0, C)
+                def _(j):
+                    @pl.when(now(j))
+                    def _():
+                        start_raw(ITERS, column(j), through=False)
+
     F[me] = jnp.sum(MOM[2 * ITERS - 1], axis=0, keepdims=True)
     spread(F, sF)
 
@@ -482,9 +496,11 @@
                 start_raw(ITERS, column(j), through=False)
 
         if paired:
-            @pl.loop(C - HOLD, C)
+            @pl.loop(0, C)
             def _(j):
-                start_raw(ITERS, column(j), own=False)
+                @pl.when((ix >= 4) | (j >= C - HOLD))
+                def _():
+                    start_raw(ITERS, column(j), own=False)
 
     @pl.loop(0, C // 2)
     def _(j):
@@ -555,13 +571,12 @@
     mask = jnp.swapaxes(mask, 1, 2)
     hbm = pl.BlockSpec(memory_space=pl.ANY)
     vmem = pl.BlockSpec(memory_space=pltpu.VMEM)
-    smem = pl.BlockSpec(memory_space=pltpu.SMEM)
     dma = pltpu.SemaphoreType.DMA
     shape = pltpu.VMEM(volt.shape, F32)
     volt, direction, res, image, step = pl.pallas_call(
         functools.partial(kernel, nx, ny, paired),
         out_shape=(shape, shape, shape, shape, pltpu.VMEM((1, S), F32)),
-        in_specs=[hbm, hbm, vmem, hbm, hbm, hbm, hbm, smem],
+        in_specs=[hbm] * 8,
         out_specs=(vmem,) * 5,
         scratch_shapes=[
             pltpu.VMEM((STEPS, R, C, B, S), F32),
@@ -581,7 +596,9 @@
             pltpu.VMEM((2 * ITERS, 8, S), F32),
             pltpu.VMEM((nx * ny, 2 * ITERS, S), F32),
             pltpu.VMEM((nx * ny, 1, S), F32),
-            dma((6,)),
+            pltpu.VMEM((R, C, B), F32),
+            pltpu.SMEM((R, 2, C), jnp.int32),
+            dma((8,)),
             dma, dma((2, C)),
             dma, dma((2, C)),
             dma, dma((2, R)),

time: 115 us -> 113 us (0.983)
  Pallas kernels: 110 us -> 108 us
    pallas_call x1, Pallas kernels: 110 us -> 108 us  [shards(): pl.pallas_call(functools.partial(kernel, nx, ny, paired), out_shape=(shap...]
where the time goes in v2:
time: 113 us; the launch traced here: 112 us
  Pallas kernels  108 us (96%)
  other arithmetic  3.24 us (3%)
    pallas_call x1, Pallas kernels, shards(): pl.pallas_call(functools.partial(kernel, nx, ny, paired), out_shape=(shap...  108 us
    sub x1, other arithmetic, shards(): return (volt + step * direction, res - step * image)  3.24 us

profile of v2, /device:TPU:0, one launch (start us, length us, event | category | flops | bytes accessed | tf_op | source)
XLA Modules:
  0.0 112.1 jit_solution(14496566140388714908)
XLA Ops:
  0.6 108.2 %shard_map.95 = (f32[4,8,128,128]{3,2,1,0:T(8,128)S(1)}, f32[4,8,128,128]{3,2,1,0:T(8,128)S(1)}, f32[4,8,128,128]{3,2,1,0:T(8,128)S(1)}, f32[4,8,128,128]{3,2,1,0:T(8,128)S(1)}, f32[1,128]{1,0:T(1,128)S(1)}) custom-call(f32[4,8,128,128]{3,2,1,0:T(8,128)} %volt.1, f32[4,8,128,128]{3,2,1,0:T(8,128)} %source.1, f32[4,8,128]{2,1,0:T(8,128)} %cap_in.1, ...), custom_call_target="tpu_custom_call" | custom-call | tf_op jit(solution)/shard_map/pallas_call | solution.py:576
  108.8 3.2 %multiply_subtract_fusion = (f32[4,8,128,128]{3,2,1,0:T(8,128)}, f32[4,8,128,128]{3,2,1,0:T(8,128)}) fusion(f32[4,8,128,128]{3,2,1,0:T(8,128)S(1)} %get-tuple-element.10, f32[4,8,128,128]{3,2,1,0:T(8,128)S(1)} %get-tuple-element.11, f32[128]{0:T(128)S(1)} %bitcast.2, f32[4,8,128,128]{3,2,1,0:T(8,128)S(1)} %get-tuple-element.7, ...), kind=kLoop, calls=%fused_computation | loop fusion | flops 2097152 | bytes 12583424 | tf_op jit(solution)/shard_map/sub | solution.py:613
